TPU v7x, 128 devices: a whole 4x4x4 slice. The times are simulated.
128 devices in a mesh: grp: 16 (over z, y), mem: 8 (over x, core).
Axes of the slice: x: 4, y: 4, z: 4, core: 2. Of those that a mesh axis runs over, the one named last changes fastest.
Arguments:
- queries: bfloat16 [32768, 2048], P(('grp', 'mem')), may hold values from -6 to 6
- keys: bfloat16 [32768, 2048], P(('grp', 'mem')), may hold values from -6 to 6
- values: bfloat16 [32768, 2048], P(('grp', 'mem')), may hold values from -6 to 6
- grad_out: bfloat16 [32768, 2048], P(('grp', 'mem')), may hold values from -0.0625 to 0.0625
- log_decay: float32 [8, 32768], P(None, ('grp', 'mem')), may hold values from -1.6 to 0
Outputs:
- grad_queries: bfloat16 [32768, 2048], P(('grp', 'mem'))
- grad_keys: bfloat16 [32768, 2048], P(('grp', 'mem'))
- grad_values: bfloat16 [32768, 2048], P(('grp', 'mem'))
All inputs are finite; a program needn't handle non-finite values.
Results may differ from a plain program's by a relative error of at most 0.0052.
Values sent between devices are 32-bit elements; how exact they have to be, the bound alone decides.
No kernel may reach another device: no remote copies, remote signals or barrier semaphores. Data moves between devices by JAX's collectives and lax.ppermute only.
A program may use at most 128 MiB of HBM per device.

v0:
```python
import jax
import jax.numpy as jnp
from jax import lax
from jax.sharding import Mesh
from jax.sharding import PartitionSpec as P

HEAD_COUNT = 8
DK = 256
DV = 256
BLOCK = 128
GRP = ("grp_0", "grp_1")
GRP_MEM = ("grp_0", "grp_1", "mem")


def filled_with(x, identity):
    return jax.tree.map(
        lambda part, zero: jnp.zeros_like(part) + jnp.asarray(zero, part.dtype), x, identity
    )


def entering(x, axes, combine, identity, reverse):
    before = start = filled_with(x, identity)
    total = x
    for axis in reversed(axes):
        length, mine = (lax.axis_size(axis), lax.axis_index(axis))
        pieces = jax.tree.map(lambda part: lax.all_gather(part, axis), total)
        inside, total = (start, start)
        for k in reversed(range(length)) if reverse else range(length):
            passed = k > mine if reverse else k < mine
            total = combine(total, jax.tree.map(lambda part: part[k], pieces))
            inside = jax.tree.map(lambda new, old: jnp.where(passed, new, old), total, inside)
        before = combine(inside, before)
    return before


def chain(earlier, later):
    early_decay, early_state = earlier
    late_decay, late_state = later
    return (early_decay * late_decay, late_state + late_decay[:, None, None] * early_state)


def body(queries, keys, values, grad_out, log_decay):
    tokens = queries.shape[0]
    count = tokens // BLOCK
    scale = DK ** (-0.5)
    query_blocks = queries.reshape(count, BLOCK, HEAD_COUNT, DK)
    key_blocks = keys.reshape(count, BLOCK, HEAD_COUNT, DK)
    value_blocks = values.reshape(count, BLOCK, HEAD_COUNT, DV)
    grad_blocks = grad_out.reshape(count, BLOCK, HEAD_COUNT, DV)
    logs = jnp.transpose(log_decay.reshape(HEAD_COUNT, count, BLOCK), (1, 0, 2))
    cumul = jnp.cumsum(logs, axis=2)
    ends = cumul[:, :, -1]
    lower = jnp.tril(jnp.ones((BLOCK, BLOCK), dtype=bool))
    spread = cumul[:, :, :, None] - cumul[:, :, None, :]
    decay = jnp.where(lower, jnp.exp(jnp.where(lower, spread, 0.0)), 0.0)
    scores = jnp.einsum(
        "bthe,bshe->bhts", grad_blocks, value_blocks, preferred_element_type=jnp.float32
    )
    weight_grad = (scores * decay).astype(jnp.bfloat16)
    attend = jnp.einsum(
        "bthd,bshd->bhts", query_blocks, key_blocks, preferred_element_type=jnp.float32
    )
    weight_value = (attend * decay).astype(jnp.bfloat16)
    inner_query = jnp.einsum(
        "bhts,bshd->bthd", weight_grad, key_blocks, preferred_element_type=jnp.float32
    )
    inner_key = jnp.einsum(
        "bhts,bthd->bshd", weight_grad, query_blocks, preferred_element_type=jnp.float32
    )
    inner_value = jnp.einsum(
        "bhts,bthe->bshe", weight_value, grad_blocks, preferred_element_type=jnp.float32
    )
    head_factor = jnp.exp(jnp.transpose(cumul, (0, 2, 1)))[..., None]
    tail_factor = jnp.exp(jnp.transpose(ends[:, :, None] - cumul, (0, 2, 1)))[..., None]
    keys_decayed = (key_blocks * tail_factor).astype(jnp.bfloat16)
    queries_decayed = (query_blocks * head_factor).astype(jnp.bfloat16)
    forward_parts = jnp.einsum(
        "bshd,bshe->bhde", keys_decayed, value_blocks, preferred_element_type=jnp.float32
    )
    reverse_parts = jnp.einsum(
        "bthd,bthe->bhde", queries_decayed, grad_blocks, preferred_element_type=jnp.float32
    )
    block_decay = jnp.exp(ends)
    running = jnp.zeros((HEAD_COUNT, DK, DV), jnp.float32)
    carried = jnp.ones((HEAD_COUNT,), jnp.float32)
    prefix_list = []
    carried_list = []
    for position in range(count):
        prefix_list.append(running)
        carried_list.append(carried)
        running = block_decay[position][:, None, None] * running + forward_parts[position]
        carried = carried * block_decay[position]
    forward_total = running
    running = jnp.zeros((HEAD_COUNT, DK, DV), jnp.float32)
    after = jnp.ones((HEAD_COUNT,), jnp.float32)
    suffix_list = [None] * count
    after_list = [None] * count
    for position in reversed(range(count)):
        suffix_list[position] = running
        after_list[position] = after
        running = block_decay[position][:, None, None] * running + reverse_parts[position]
        after = after * block_decay[position]
    members = lax.axis_size("mem")
    decay_cols = jnp.broadcast_to(carried[None, :, None, None], (1, HEAD_COUNT, members, 1))
    pieces = (
        lax.all_to_all(decay_cols, "mem", split_axis=2, concat_axis=0, tiled=True),
        lax.all_to_all(forward_total[None], "mem", split_axis=2, concat_axis=0, tiled=True),
        lax.all_to_all(running[None], "mem", split_axis=2, concat_axis=0, tiled=True),
    )
    member_decays = pieces[0][:, :, 0, 0]
    width = DK // members
    share_identity = (
        jnp.ones((HEAD_COUNT,), jnp.float32),
        jnp.zeros((HEAD_COUNT, width, DV), jnp.float32),
    )
    forward_prefix = []
    accum = share_identity
    for index in range(members):
        forward_prefix.append(accum)
        accum = chain(accum, (member_decays[index], pieces[1][index]))
    forward_whole = accum
    reverse_prefix = [None] * members
    accum = share_identity
    for index in reversed(range(members)):
        reverse_prefix[index] = accum
        accum = chain(accum, (member_decays[index], pieces[2][index]))
    group_first = entering(forward_whole, GRP, chain, share_identity, False)
    group_second = entering(accum, GRP, chain, share_identity, True)
    first_stack = jnp.stack(
        [chain(group_first, forward_prefix[index])[1] for index in range(members)]
    )
    second_stack = jnp.stack(
        [chain(group_second, reverse_prefix[index])[1] for index in range(members)]
    )
    returned = (
        lax.all_to_all(first_stack, "mem", split_axis=0, concat_axis=2, tiled=True),
        lax.all_to_all(second_stack, "mem", split_axis=0, concat_axis=2, tiled=True),
    )
    state_from = returned[0][0]
    grads_from = returned[1][0]
    states_low = (
        jnp.stack(prefix_list) + jnp.stack(carried_list)[:, :, None, None] * state_from[None]
    ).astype(jnp.bfloat16)
    grads_low = (
        jnp.stack(suffix_list) + jnp.stack(after_list)[:, :, None, None] * grads_from[None]
    ).astype(jnp.bfloat16)
    outer_query = jnp.einsum(
        "bthe,bhde->bthd", grad_blocks, states_low, preferred_element_type=jnp.float32
    )
    outer_key = jnp.einsum(
        "bshe,bhde->bshd", value_blocks, grads_low, preferred_element_type=jnp.float32
    )
    outer_value = jnp.einsum(
        "bshd,bhde->bshe", key_blocks, grads_low, preferred_element_type=jnp.float32
    )
    grad_queries = (scale * (inner_query + head_factor * outer_query)).astype(jnp.bfloat16)
    grad_keys = (scale * (inner_key + tail_factor * outer_key)).astype(jnp.bfloat16)
    grad_values = (scale * (inner_value + tail_factor * outer_value)).astype(jnp.bfloat16)
    return (
        grad_queries.reshape(tokens, HEAD_COUNT * DK),
        grad_keys.reshape(tokens, HEAD_COUNT * DK),
        grad_values.reshape(tokens, HEAD_COUNT * DV),
    )


def solution(mesh):
    torus = Mesh(mesh.devices.reshape(4, 4, mesh.shape["mem"]), ("grp_0", "grp_1", "mem"))
    return jax.shard_map(
        body,
        mesh=torus,
        in_specs=(
            P(GRP_MEM, None),
            P(GRP_MEM, None),
            P(GRP_MEM, None),
            P(GRP_MEM, None),
            P(None, GRP_MEM),
        ),
        out_specs=(P(GRP_MEM, None), P(GRP_MEM, None), P(GRP_MEM, None)),
        check_vma=False,
    )
```

profile of v0, /device:TPU:1, one launch (start us, length us, event | category | flops | bytes accessed | tf_op | source)
XLA Modules:
  0.0 245.2 jit_solution(16652471330811321693)
XLA Ops:
  9.3 5.8 %all-to-all-start.1 = ((f32[1,8,8,1]{1,3,0,2:T(1,128)}), f32[1,8,8,1]{1,3,0,2:T(1,128)S(1)}, u32[]{:S(2)}, u32[]{:S(2)}) async-start(f32[1,8,8,1]{1,3,0,2:T(1,128)} %broadcast_in_dim.20), calls=%async_computation.1 | async-start | bytes 8192 | tf_op jit(solution)/shard_map/all_to_all | solution.py:106
  22.4 2.9 %slice_add_fusion = (f32[1,8,256,256]{3,2,1,0:T(8,128)S(1)}, f32[1,8,256,256]{3,2,1,0:T(8,128)S(1)}, f32[1,8,256,256]{3,2,1,0:T(8,128)}, f32[1,8,256,256]{3,2,1,0:T(8,128)}) fusion(f32[2,8,256,256]{3,2,1,0:T(8,128)S(1)} %fusion.15, f32[8]{0:T(128)S(1)} %get-tuple-element.70, f32[8]{0:T(128)S(1)} %get-tuple-element.73, f32[2,8,256,256]{3,2,1,0:T(8,128)S(1)} %fusion.14, ...), kind=kLoop, calls=%fused_computation.3 | loop fusion | flops 3145728 | bytes 16777344 | tf_op jit(solution)/shard_map/add | solution.py:101
  25.2 2.6 %copy.204 = f32[1,8,256,256]{3,1,0,2:T(8,128)} copy(f32[1,8,256,256]{3,2,1,0:T(8,128)S(1)} %get-tuple-element.23) | data formatting | bytes 4194304 | tf_op jit(solution)/shard_map/add | solution.py:101
  27.8 4.8 %all-to-all-start.3 = ((f32[1,8,256,256]{3,1,0,2:T(8,128)}), f32[1,8,256,256]{3,1,0,2:T(8,128)}, u32[]{:S(2)}, u32[]{:S(2)}) async-start(f32[1,8,256,256]{3,1,0,2:T(8,128)} %copy.204), calls=%async_computation.3 | async-start | bytes 4194304 | tf_op jit(solution)/shard_map/all_to_all | solution.py:108
  32.6 4.1 %copy.185 = f32[1,8,256,256]{3,1,0,2:T(8,128)} copy(f32[1,8,256,256]{3,2,1,0:T(8,128)} %get-tuple-element.78) | data formatting | bytes 4194304 | tf_op jit(solution)/shard_map/add | solution.py:91
  36.9 22.1 %all-to-all-done.3 = f32[1,8,256,256]{3,1,0,2:T(8,128)} async-done(((f32[1,8,256,256]{3,1,0,2:T(8,128)}), f32[1,8,256,256]{3,1,0,2:T(8,128)}, u32[]{:S(2)}, u32[]{:S(2)}) %all-to-all-start.3) | async-done | bytes 2097184 | tf_op jit(solution)/shard_map/all_to_all | solution.py:108
  58.9 5.2 %all-to-all-start = ((f32[1,8,256,256]{3,1,0,2:T(8,128)}), f32[1,8,256,256]{3,1,0,2:T(8,128)}, u32[]{:S(2)}, u32[]{:S(2)}) async-start(f32[1,8,256,256]{3,1,0,2:T(8,128)} %copy.185), calls=%async_computation | async-start | bytes 4194304 | tf_op jit(solution)/shard_map/all_to_all | solution.py:107
  65.0 2.2 copy.278
  69.8 20.7 %all-to-all-done = f32[1,8,256,256]{3,1,0,2:T(8,128)} async-done(((f32[1,8,256,256]{3,1,0,2:T(8,128)}), f32[1,8,256,256]{3,1,0,2:T(8,128)}, u32[]{:S(2)}, u32[]{:S(2)}) %all-to-all-start) | async-done | bytes 2097184 | tf_op jit(solution)/shard_map/all_to_all | solution.py:107
  90.5 2.3 copy.186
  95.2 7.9 %all-gather.2 = f32[4,1,8]{2,1,0:T(1,128)S(1)} all-gather(f32[1,1,8]{2,1,0:T(1,128)S(1)} %get-tuple-element.41), channel_id=1, replica_groups=mesh['grp_0'=4,'grp_1'=4,'mem'=8] {'grp_1'}, dimensions={0}, use_global_device_ids=true | all-gather | bytes 160 | tf_op jit(solution)/shard_map/all_gather | solution.py:26
  103.2 2.0 slice_add_fusion.11
  105.4 5.2 %all-gather = f32[4,1,8]{2,1,0:T(1,128)S(1)} all-gather(f32[1,1,8]{2,1,0:T(1,128)S(1)} %get-tuple-element.42), channel_id=1, replica_groups=mesh['grp_0'=4,'grp_1'=4,'mem'=8] {'grp_1'}, dimensions={0}, use_global_device_ids=true | all-gather | bytes 160 | tf_op jit(solution)/shard_map/all_gather | solution.py:26
  110.6 9.4 %all-gather.1 = f32[4,1,8]{2,1,0:T(1,128)S(1)} all-gather(f32[1,1,8]{2,1,0:T(1,128)S(1)} %get-tuple-element.66), channel_id=1, replica_groups=mesh['grp_0'=4,'grp_1'=4,'mem'=8] {'grp_0'}, dimensions={0}, use_global_device_ids=true | all-gather | bytes 160 | tf_op jit(solution)/shard_map/all_gather | solution.py:26
  120.0 5.4 %all-gather.3 = f32[4,1,8]{2,1,0:T(1,128)S(1)} all-gather(f32[1,1,8]{2,1,0:T(1,128)S(1)} %get-tuple-element.56), channel_id=1, replica_groups=mesh['grp_0'=4,'grp_1'=4,'mem'=8] {'grp_0'}, dimensions={0}, use_global_device_ids=true | all-gather | bytes 160 | tf_op jit(solution)/shard_map/all_gather | solution.py:26
  126.5 2.0 slice_add_fusion.19
  128.6 18.7 %all-gather.15.cloned.1.call-done = f32[4,8,32,256]{3,2,1,0:T(8,128)} async-done(((f32[1,8,32,256]{3,2,1,0:T(8,128)}), f32[4,8,32,256]{3,2,1,0:T(8,128)}) %all-gather.15.cloned.1.call-update) | async-done | bytes 1048592 | tf_op jit(solution)/shard_map/all_gather | solution.py:26
  147.3 2.8 %add_dynamic-update-slice_fusion.6 = (f32[8,8,32,256]{3,2,1,0:T(8,128)}, f32[1,8,32,256]{3,2,1,0:T(8,128)S(1)}) fusion(f32[8]{0:T(128)S(1)} %get-tuple-element.13, f32[1,8,32,256]{3,2,1,0:T(8,128)} %get-tuple-element.20, f32[8]{0:T(128)S(1)} %get-tuple-element.5, f32[8,1,8,32,256]{4,3,2,1,0:T(8,128)} %bitcast.342, pred[]{:T(512)S(6)} %lt.31, pred[]{:T(512)S(6)} %lt.30, ...), kind=kLoop, calls=%fused_computation.113 | loop fusion | flops 1835007 | bytes 3146088
  156.8 1.8 add_dynamic-update-slice_fusion
  159.3 7.0 %all-to-all-start.4 = ((f32[8,8,32,256]{3,2,1,0:T(8,128)}), f32[8,8,32,256]{3,2,1,0:T(8,128)}, u32[]{:S(2)}, u32[]{:S(2)}) async-start(f32[8,8,32,256]{3,2,1,0:T(8,128)} %constant_dynamic-update-slice_fusion.1), calls=%async_computation.4 | async-start | bytes 4194304 | tf_op jit(solution)/shard_map/all_to_all | solution.py:137
  166.3 7.9 %all-gather.11.cloned.1.call-done = f32[4,8,32,256]{3,2,1,0:T(8,128)} async-done(((f32[1,8,32,256]{3,2,1,0:T(8,128)}), f32[4,8,32,256]{3,2,1,0:T(8,128)}) %all-gather.11.cloned.1.call-update) | async-done | bytes 1048592 | tf_op jit(solution)/shard_map/all_gather | solution.py:26
  174.3 2.7 %constant_dynamic-update-slice_fusion = (f32[8,8,32,256]{3,2,1,0:T(8,128)}, f32[1,8,32,256]{3,2,1,0:T(8,128)S(1)}) fusion(pred[]{:T(512)S(6)} %gt.31, pred[]{:T(512)S(6)} %gt.30, pred[]{:T(512)S(6)} %gt.29, f32[8]{0:T(128)S(1)} %copy-done.30, f32[4,8,32,256]{3,2,1,0:T(8,128)} %all-gather.11.cloned.1.call-done, f32[8]{0:T(128)S(1)} %copy-done.28, ...), kind=kLoop, calls=%fused_computation.122 | loop fusion | flops 1572863 | bytes 2621736
  182.7 10.0 %all-to-all-done.4 = f32[8,8,32,256]{3,2,1,0:T(8,128)} async-done(((f32[8,8,32,256]{3,2,1,0:T(8,128)}), f32[8,8,32,256]{3,2,1,0:T(8,128)}, u32[]{:S(2)}, u32[]{:S(2)}) %all-to-all-start.4) | async-done | bytes 2097184 | tf_op jit(solution)/shard_map/all_to_all | solution.py:137
  192.6 5.2 %all-to-all-start.2 = ((f32[8,8,32,256]{3,2,1,0:T(8,128)}), f32[8,8,32,256]{3,2,1,0:T(8,128)}, u32[]{:S(2)}, u32[]{:S(2)}) async-start(f32[8,8,32,256]{3,2,1,0:T(8,128)} %add_dynamic-update-slice_fusion.7), calls=%async_computation.2 | async-start | bytes 4194304 | tf_op jit(solution)/shard_map/all_to_all | solution.py:136
  197.9 3.0 %fusion.12 = bf16[2,8,128,128]{3,2,1,0:T(8,128)(2,1)} fusion(bf16[2,128,8,256]{3,2,1,0:T(8,128)(2,1)} %bitcast.354, bf16[2,128,8,256]{3,2,1,0:T(8,128)(2,1)} %bitcast.350, f32[2,8,128]{2,1,0:T(8,128)S(1)} %reduce_window_sum.11, pred[128,128]{1,0:T(8,128)(4,1)S(1)} %iota_compare_fusion), kind=kOutput, calls=%fused_computation.26 | convolution fusion | flops 135528448 | bytes 2646016 | tf_op jit(solution)/shard_map/bthe,bshe->bhts/dot_general | solution.py:56
  200.8 1.8 copy.207
  202.7 2.4 fusion.22
  205.1 2.1 fusion.26
  207.2 17.0 %all-to-all-done.2 = f32[8,8,32,256]{3,2,1,0:T(8,128)} async-done(((f32[8,8,32,256]{3,2,1,0:T(8,128)}), f32[8,8,32,256]{3,2,1,0:T(8,128)}, u32[]{:S(2)}, u32[]{:S(2)}) %all-to-all-start.2) | async-done | bytes 2097184 | tf_op jit(solution)/shard_map/all_to_all | solution.py:136
  224.2 1.9 copy.195
  232.4 3.2 %fusion.3 = bf16[2,128,8,256]{3,1,2,0:T(8,128)(2,1)} fusion(f32[2,8,256,128]{2,3,1,0:T(8,128)} %fusion.26, f32[2,128,8]{1,2,0:T(8,128)S(1)} %get-tuple-element.40, bf16[2,128,8,256]{3,2,1,0:T(8,128)(2,1)S(1)} %bitcast.348, bf16[2,128,8,256]{3,2,1,0:T(8,128)(2,1)S(1)} %bitcast.335, bf16[2,128,8,256]{3,2,1,0:T(8,128)(2,1)S(1)} %bitcast.352, ...), kind=kOutput, calls=%fused_computation.10 | convolution fusion | flops 271843328 | bytes 6324224 | tf_op jit(solution)/shard_map/bhts,bthe->bshe/dot_general | solution.py:70
  235.6 1.8 copy.218
  (122 shorter events, 37.3 us)
Async XLA Ops:
  7.2 10.1 %copy-start.17 = (bf16[256,2048]{1,0:T(8,128)(2,1)S(1)}, bf16[256,2048]{1,0:T(8,128)(2,1)}, u32[]{:S(2)}) copy-start(bf16[256,2048]{1,0:T(8,128)(2,1)} %param.8) | copy-start | bytes 3145732
  9.3 18.5 %all-to-all-start.1 = ((f32[1,8,8,1]{1,3,0,2:T(1,128)}), f32[1,8,8,1]{1,3,0,2:T(1,128)S(1)}, u32[]{:S(2)}, u32[]{:S(2)}) async-start(f32[1,8,8,1]{1,3,0,2:T(1,128)} %broadcast_in_dim.20), calls=%async_computation.1 | async-start | bytes 8192 | tf_op jit(solution)/shard_map/all_to_all | solution.py:106
  17.3 2.3 copy-start.3
  17.6 2.0 copy-start.5
  18.0 3.0 %copy-start.7 = (bf16[32,8,8,256]{3,2,1,0:T(8,128)(2,1)}, bf16[32,8,8,256]{3,2,1,0:T(8,128)(2,1)S(1)}, u32[]{:S(2)}) copy-start(bf16[32,8,8,256]{3,2,1,0:T(8,128)(2,1)S(1)} %copy.237) | copy-start | bytes 3145732
  27.8 31.1 %all-to-all-start.3 = ((f32[1,8,256,256]{3,1,0,2:T(8,128)}), f32[1,8,256,256]{3,1,0,2:T(8,128)}, u32[]{:S(2)}, u32[]{:S(2)}) async-start(f32[1,8,256,256]{3,1,0,2:T(8,128)} %copy.204), calls=%async_computation.3 | async-start | bytes 4194304 | tf_op jit(solution)/shard_map/all_to_all | solution.py:108
  58.9 31.5 %all-to-all-start = ((f32[1,8,256,256]{3,1,0,2:T(8,128)}), f32[1,8,256,256]{3,1,0,2:T(8,128)}, u32[]{:S(2)}, u32[]{:S(2)}) async-start(f32[1,8,256,256]{3,1,0,2:T(8,128)} %copy.185), calls=%async_computation | async-start | bytes 4194304 | tf_op jit(solution)/shard_map/all_to_all | solution.py:107
  64.1 39.1 %all-gather.13.cloned.1.call-start = ((), (), s32[]{:S(2)}) async-start(), calls=%async_computation.7 | async-start | bytes 1310720 | tf_op jit(solution)/shard_map/all_gather | solution.py:26
  69.8 56.7 %all-gather.9.cloned.1.call-start = ((), (), s32[]{:S(2)}) async-start(), calls=%async_computation.5 | async-start | bytes 1310720 | tf_op jit(solution)/shard_map/all_gather | solution.py:26
  95.2 52.1 %all-gather.15.cloned.1.call-start = ((), (), s32[]{:S(2)}) async-start(), calls=%async_computation.8 | async-start | bytes 1310720 | tf_op jit(solution)/shard_map/all_gather | solution.py:26
  105.3 68.9 %all-gather.11.cloned.1.call-start = ((), (), s32[]{:S(2)}) async-start(), calls=%async_computation.6 | async-start | bytes 1310720 | tf_op jit(solution)/shard_map/all_gather | solution.py:26
  147.3 2.8 %copy-start.15 = (f32[1,8,32,256]{3,2,1,0:T(8,128)S(1)}, f32[1,8,32,256]{3,2,1,0:T(8,128)}, u32[]{:S(2)}) copy-start(f32[1,8,32,256]{3,2,1,0:T(8,128)} %get-tuple-element.20) | copy-start | bytes 786436
  147.3 4.3 %copy-start.14 = (f32[1,8,32,256]{3,2,1,0:T(8,128)S(1)}, f32[1,8,32,256]{3,2,1,0:T(8,128)}, u32[]{:S(2)}) copy-start(f32[1,8,32,256]{3,2,1,0:T(8,128)} %get-tuple-element.21) | copy-start | bytes 786436
  147.3 6.0 %copy-start.25 = (f32[8]{0:T(128)S(1)}, f32[8]{0:T(128)}, u32[]{:S(2)}) copy-start(f32[8]{0:T(128)} %get-tuple-element.16) | copy-start | bytes 100
  150.1 4.1 %copy-start.13 = (f32[1,8,32,256]{3,2,1,0:T(8,128)S(1)}, f32[1,8,32,256]{3,2,1,0:T(8,128)}, u32[]{:S(2)}) copy-start(f32[1,8,32,256]{3,2,1,0:T(8,128)} %get-tuple-element.22) | copy-start | bytes 786436
  150.1 5.8 %copy-start.24 = (f32[8]{0:T(128)S(1)}, f32[8]{0:T(128)}, u32[]{:S(2)}) copy-start(f32[8]{0:T(128)} %get-tuple-element.18) | copy-start | bytes 100
  159.3 15.0 %copy-start.26 = (f32[8]{0:T(128)S(1)}, f32[8]{0:T(128)}, u32[]{:S(2)}) copy-start(f32[8]{0:T(128)} %get-tuple-element.59) | copy-start | bytes 100
  159.3 15.0 %copy-start.27 = (f32[8]{0:T(128)S(1)}, f32[8]{0:T(128)}, u32[]{:S(2)}) copy-start(f32[8]{0:T(128)} %get-tuple-element.61) | copy-start | bytes 100
  159.3 15.0 %copy-start.28 = (f32[8]{0:T(128)S(1)}, f32[8]{0:T(128)}, u32[]{:S(2)}) copy-start(f32[8]{0:T(128)} %get-tuple-element.62) | copy-start | bytes 100
  159.3 15.0 %copy-start.29 = (f32[8]{0:T(128)S(1)}, f32[8]{0:T(128)}, u32[]{:S(2)}) copy-start(f32[8]{0:T(128)} %get-tuple-element.63) | copy-start | bytes 100
  159.3 15.0 %copy-start.30 = (f32[8]{0:T(128)S(1)}, f32[8]{0:T(128)}, u32[]{:S(2)}) copy-start(f32[8]{0:T(128)} %get-tuple-element.64) | copy-start | bytes 100
  159.3 33.3 %all-to-all-start.4 = ((f32[8,8,32,256]{3,2,1,0:T(8,128)}), f32[8,8,32,256]{3,2,1,0:T(8,128)}, u32[]{:S(2)}, u32[]{:S(2)}) async-start(f32[8,8,32,256]{3,2,1,0:T(8,128)} %constant_dynamic-update-slice_fusion.1), calls=%async_computation.4 | async-start | bytes 4194304 | tf_op jit(solution)/shard_map/all_to_all | solution.py:137
  166.3 11.5 %copy-start.23 = (f32[8]{0:T(128)S(1)}, f32[8]{0:T(128)}, u32[]{:S(2)}) copy-start(f32[8]{0:T(128)} %get-tuple-element.48) | copy-start | bytes 100
  174.2 2.8 %copy-start.1 = (f32[1,8,256,256]{3,2,1,0:T(8,128)S(1)}, f32[1,8,256,256]{3,2,1,0:T(8,128)}, u32[]{:S(2)}) copy-start(f32[1,8,256,256]{3,2,1,0:T(8,128)} %copy-done) | copy-start | bytes 6291460
  174.2 3.6 %copy-start.12 = (f32[1,8,32,256]{3,2,1,0:T(8,128)S(1)}, f32[1,8,32,256]{3,2,1,0:T(8,128)}, u32[]{:S(2)}) copy-start(f32[1,8,32,256]{3,2,1,0:T(8,128)} %get-tuple-element.36) | copy-start | bytes 786436
  174.3 5.2 %copy-start.11 = (f32[1,8,32,256]{3,2,1,0:T(8,128)S(1)}, f32[1,8,32,256]{3,2,1,0:T(8,128)}, u32[]{:S(2)}) copy-start(f32[1,8,32,256]{3,2,1,0:T(8,128)} %get-tuple-element.35) | copy-start | bytes 786436
  174.3 5.2 %copy-start.22 = (f32[8]{0:T(128)S(1)}, f32[8]{0:T(128)}, u32[]{:S(2)}) copy-start(f32[8]{0:T(128)} %get-tuple-element.46) | copy-start | bytes 100
  177.0 4.0 %copy-start.21 = (f32[8]{0:T(128)S(1)}, f32[8]{0:T(128)}, u32[]{:S(2)}) copy-start(f32[8]{0:T(128)} %get-tuple-element.44) | copy-start | bytes 100
  182.7 15.2 %copy-start.20 = (f32[1,8]{1,0:T(1,128)S(1)}, f32[1,8]{1,0:T(1,128)}, u32[]{:S(2)}) copy-start(f32[1,8]{1,0:T(1,128)} %get-tuple-element.72) | copy-start | bytes 100
  192.6 31.5 %all-to-all-start.2 = ((f32[8,8,32,256]{3,2,1,0:T(8,128)}), f32[8,8,32,256]{3,2,1,0:T(8,128)}, u32[]{:S(2)}, u32[]{:S(2)}) async-start(f32[8,8,32,256]{3,2,1,0:T(8,128)} %add_dynamic-update-slice_fusion.7), calls=%async_computation.2 | async-start | bytes 4194304 | tf_op jit(solution)/shard_map/all_to_all | solution.py:136
  207.2 18.9 %copy-start.6 = (bf16[32,8,8,256]{3,2,1,0:T(8,128)(2,1)S(1)}, bf16[32,8,8,256]{3,2,1,0:T(8,128)(2,1)}, u32[]{:S(2)}) copy-start(bf16[32,8,8,256]{3,2,1,0:T(8,128)(2,1)} %copy-done.5) | copy-start | bytes 3145732
  224.2 2.2 copy-start.9
  (8 other events, 13.4 us)
Sparse Core Ops, SparseCore 0:
  69.9 24.2 all-gather.12
  96.4 24.4 all-gather.8
  122.6 24.6 all-gather.14
  149.4 24.7 all-gather.10
where the time goes:
time: 246 us; the launch traced here: 245 us
  waiting for transfers between devices  96.4 us (39%)
  other arithmetic  31.9 us (13%)
  local copies, waits for them, and re-layouts  31.4 us (13%)
  starting transfers between devices  28.1 us (11%)
  blocking collectives  27.9 us (11%)
  matrix products  15.4 us (6%)
  between operations  14.1 us (6%)
    all_gather x4, blocking collectives, entering(): pieces = jax.tree.map(lambda part: lax.all_gather(part, axis), total)  27.9 us
    all_gather x4, waiting for transfers between devices, entering(): pieces = jax.tree.map(lambda part: lax.all_gather(part, axis), total)  26.7 us
    all_to_all x1, waiting for transfers between devices, body(): lax.all_to_all(running[None], 'mem', split_axis=2, concat_axis=0, tiled=T...  22.1 us
    all_to_all x1, waiting for transfers between devices, body(): lax.all_to_all(forward_total[None], 'mem', split_axis=2, concat_axis=0, t...  20.7 us
    unnamed x15, other arithmetic  18.8 us
    all_to_all x1, waiting for transfers between devices, body(): lax.all_to_all(first_stack, 'mem', split_axis=0, concat_axis=2, tiled=True)  17 us
    unnamed x69, local copies, waits for them, and re-layouts  11.1 us
    all_to_all x1, waiting for transfers between devices, body(): lax.all_to_all(second_stack, 'mem', split_axis=0, concat_axis=2, tiled=True)  9.97 us
  transfers between devices with their start and end apart: 9, of which 6 were waited for; matrix products, arithmetic and copies ran while one was open for 24% of the time, Pallas kernels for 0%

commit v1 on v0

v1 whole, which is shorter than its diff:
```python
import jax
import jax.numpy as jnp
from jax import lax
from jax.experimental import pallas as pl
from jax.experimental.pallas import tpu as pltpu
from jax.sharding import Mesh
from jax.sharding import PartitionSpec as P

HEADS = 8
GROUP = 4
D = 256
TOK = 256
CHIPS = ("z", "y", "x")
ALL = ("z", "y", "x", "core")
F32 = jnp.float32
BF16 = jnp.bfloat16
STATE_ROWS = 2 * D + 8


def dot(a, b, ca, cb):
    return lax.dot_general(a, b, (((ca,), (cb,)), ((), ())), preferred_element_type=F32)


def exact_dot(a, b, ca, cb):
    return lax.dot_general(
        a,
        b,
        (((ca,), (cb,)), ((), ())),
        preferred_element_type=F32,
        precision=lax.Precision.HIGHEST,
    )


def lower_mask():
    rows = lax.broadcasted_iota(jnp.int32, (TOK, TOK), 0)
    cols = lax.broadcasted_iota(jnp.int32, (TOK, TOK), 1)
    return cols <= rows


def pick_column(table, head):
    lanes = lax.broadcasted_iota(jnp.int32, table.shape, 1)
    return jnp.sum(jnp.where(lanes == head, table, 0.0), axis=1, keepdims=True)


def states_kernel(grp_ref, log_ref, q_ref, k_ref, v_ref, g_ref, out_ref, col_ref):
    step = pl.program_id(0)

    @pl.when(step == 0)
    def _():
        tri = jnp.where(lower_mask(), 1.0, 0.0)
        col_ref[...] = exact_dot(tri, log_ref[...], 1, 1)

    head = grp_ref[0] * GROUP + step
    cumul = pick_column(col_ref[...], head)
    end = cumul[TOK - 1 : TOK, :]
    keys = (k_ref[...].astype(F32) * jnp.exp(end - cumul)).astype(BF16)
    queries = (q_ref[...].astype(F32) * jnp.exp(cumul)).astype(BF16)
    out_ref[0, 0:D, :] = dot(keys, v_ref[...], 0, 0)
    out_ref[0, D : 2 * D, :] = dot(queries, g_ref[...], 0, 0)
    out_ref[0, 2 * D : STATE_ROWS, :] = jnp.broadcast_to(jnp.exp(end), (8, D))


def head_spec():
    return pl.BlockSpec((TOK, D), lambda i, grp: (0, grp[0] * GROUP + i))


def whole(shape):
    return pl.BlockSpec(shape, lambda i, grp: (0,) * len(shape))


def device_states(grp, log_decay, q, k, v, g):
    return pl.pallas_call(
        states_kernel,
        out_shape=jax.ShapeDtypeStruct((GROUP, STATE_ROWS, D), F32),
        grid_spec=pltpu.PrefetchScalarGridSpec(
            num_scalar_prefetch=1,
            grid=(GROUP,),
            in_specs=[whole((HEADS, TOK))] + [head_spec()] * 4,
            out_specs=pl.BlockSpec((1, STATE_ROWS, D), lambda i, grp: (i, 0, 0)),
            scratch_shapes=[pltpu.VMEM((TOK, HEADS), F32)],
        ),
        name="device_states",
    )(grp, log_decay, q, k, v, g)


def combine_kernel(core_ref, own_ref, other_ref, out_ref):
    first = core_ref[0] == 0
    own_decay = own_ref[0, 2 * D : 2 * D + 1, 0:128]
    other_decay = other_ref[0, 2 * D : 2 * D + 1, 0:128]
    one = jnp.ones_like(own_decay)
    fwd_own = jnp.where(first, other_decay, one)
    fwd_other = jnp.where(first, one, own_decay)
    rev_own = jnp.where(first, one, other_decay)
    rev_other = jnp.where(first, own_decay, one)
    for half in range(2):
        lanes = slice(128 * half, 128 * half + 128)
        fwd = fwd_own * own_ref[0, 0:D, lanes] + fwd_other * other_ref[0, 0:D, lanes]
        rev = rev_own * own_ref[0, D : 2 * D, lanes] + rev_other * other_ref[0, D : 2 * D, lanes]
        out_ref[:, 16 * half : 16 * half + 16, :] = fwd.reshape(16, 16, 128)
        out_ref[:, 32 + 16 * half : 48 + 16 * half, :] = rev.reshape(16, 16, 128)
    out_ref[:, 64:72, :] = jnp.broadcast_to((own_decay * other_decay)[None], (16, 8, 128))


def combine(core, own, other):
    state = pl.BlockSpec((1, STATE_ROWS, D), lambda i, core: (i, 0, 0))
    return pl.pallas_call(
        combine_kernel,
        out_shape=jax.ShapeDtypeStruct((64, 72, 128), F32),
        grid_spec=pltpu.PrefetchScalarGridSpec(
            num_scalar_prefetch=1,
            grid=(GROUP,),
            in_specs=[state, state],
            out_specs=pl.BlockSpec((16, 72, 128), lambda i, core: (i, 0, 0)),
        ),
        name="combine_cores",
    )(core, own, other)


def scan_kernel(in_ref, out_ref):
    def fwd_step(chip, carry):
        out_ref[chip, 0:32, :] = carry
        decay = in_ref[chip, 64:65, :]
        return decay * carry + in_ref[chip, 0:32, :]

    def rev_step(index, carry):
        chip = 63 - index
        out_ref[chip, 32:64, :] = carry
        decay = in_ref[chip, 64:65, :]
        return decay * carry + in_ref[chip, 32:64, :]

    def both(index, carry):
        return fwd_step(index, carry[0]), rev_step(index, carry[1])

    zero = jnp.zeros((32, 128), F32)
    lax.fori_loop(0, 64, both, (zero, zero), unroll=8)


def scan_chips(received):
    return pl.pallas_call(
        scan_kernel,
        out_shape=jax.ShapeDtypeStruct((64, 64, 128), F32),
        in_specs=[pl.BlockSpec(memory_space=pltpu.VMEM)],
        out_specs=pl.BlockSpec(memory_space=pltpu.VMEM),
        name="scan_chips",
    )(received)


def middle_kernel(core_ref, back_ref, own_ref, other_ref, keep_ref, send_ref):
    first = core_ref[0] == 0
    own_decay = own_ref[0, 2 * D : 2 * D + 1, 0:128]
    other_decay = other_ref[0, 2 * D : 2 * D + 1, 0:128]
    fwd_decay = jnp.where(first, own_decay, other_decay)
    rev_decay = jnp.where(first, other_decay, own_decay)
    for half in range(2):
        lanes = slice(128 * half, 128 * half + 128)
        fwd_enter = back_ref[:, 16 * half : 16 * half + 16, :].reshape(D, 128)
        rev_enter = back_ref[:, 32 + 16 * half : 48 + 16 * half, :].reshape(D, 128)
        fwd_part = jnp.where(first, own_ref[0, 0:D, lanes], other_ref[0, 0:D, lanes])
        rev_part = jnp.where(first, other_ref[0, D : 2 * D, lanes], own_ref[0, D : 2 * D, lanes])
        fwd_mid = fwd_decay * fwd_enter + fwd_part
        rev_mid = rev_decay * rev_enter + rev_part
        keep_ref[0, 0:D, lanes] = jnp.where(first, fwd_enter, fwd_mid)
        keep_ref[0, D : 2 * D, lanes] = jnp.where(first, rev_mid, rev_enter)
        send_ref[0, 0:D, lanes] = jnp.where(first, fwd_mid, fwd_enter)
        send_ref[0, D : 2 * D, lanes] = jnp.where(first, rev_enter, rev_mid)


def middle(core, back, own, other):
    state = pl.BlockSpec((1, STATE_ROWS, D), lambda i, core: (i, 0, 0))
    pair = pl.BlockSpec((1, 2 * D, D), lambda i, core: (i, 0, 0))
    return pl.pallas_call(
        middle_kernel,
        out_shape=[jax.ShapeDtypeStruct((GROUP, 2 * D, D), F32)] * 2,
        grid_spec=pltpu.PrefetchScalarGridSpec(
            num_scalar_prefetch=1,
            grid=(GROUP,),
            in_specs=[pl.BlockSpec((16, 64, 128), lambda i, core: (i, 0, 0)), state, state],
            out_specs=[pair, pair],
        ),
        name="middle_states",
    )(core, back, own, other)


def grads_kernel(grp_ref, log_ref, q_ref, k_ref, v_ref, g_ref, st_ref, *rest):
    gq_ref, gk_ref, gv_ref, col_ref, row_ref = rest[-5:]
    step = pl.program_id(0)

    @pl.when(step == 0)
    def _():
        tri = jnp.where(lower_mask(), 1.0, 0.0)
        col_ref[...] = exact_dot(tri, log_ref[...], 1, 1)
        row_ref[...] = exact_dot(log_ref[...], tri, 1, 1)

    head = grp_ref[0] * GROUP + step
    scale = D ** (-0.5)
    col = pick_column(col_ref[...], head)
    row = row_ref[pl.ds(head, 1), :]
    lower = lower_mask()
    decay = jnp.where(lower, jnp.exp(jnp.where(lower, col - row, 0.0)), 0.0)
    head_factor = jnp.exp(col)
    tail_factor = jnp.exp(col[TOK - 1 : TOK, :] - col)
    q, k, v, g = q_ref[...], k_ref[...], v_ref[...], g_ref[...]
    fwd = st_ref[0, 0:D, :].astype(BF16)
    rev = st_ref[0, D : 2 * D, :].astype(BF16)
    weight_grad = (dot(g, v, 1, 1) * decay).astype(BF16)
    weight_value = (dot(q, k, 1, 1) * decay).astype(BF16)
    gq = dot(weight_grad, k, 1, 0) + head_factor * dot(g, fwd, 1, 1)
    gq_ref[...] = (scale * gq).astype(BF16)
    gk = dot(weight_grad, q, 0, 0) + tail_factor * dot(v, rev, 1, 1)
    gk_ref[...] = (scale * gk).astype(BF16)
    gv = dot(weight_value, g, 0, 0) + tail_factor * dot(k, rev, 1, 0)
    gv_ref[...] = (scale * gv).astype(BF16)


def gradients(grp, log_decay, q, k, v, g, states, started=()):
    shape = jax.ShapeDtypeStruct((TOK, HEADS * D), BF16)
    count = len(started)
    return pl.pallas_call(
        grads_kernel,
        out_shape=[shape] * 3,
        grid_spec=pltpu.PrefetchScalarGridSpec(
            num_scalar_prefetch=1,
            grid=(GROUP,),
            in_specs=[whole((HEADS, TOK))]
            + [head_spec()] * 4
            + [pl.BlockSpec((1, 2 * D, D), lambda i, grp: (i, 0, 0))]
            + [pl.BlockSpec(memory_space=pl.ANY)] * count,
            out_specs=[head_spec()] * 3,
            scratch_shapes=[pltpu.VMEM((TOK, HEADS), F32), pltpu.VMEM((HEADS, TOK), F32)],
        ),
        input_output_aliases={7 + n: n for n in range(count)},
        name="gradients",
    )(grp, log_decay, q, k, v, g, states, *started)


def body(queries, keys, values, grad_out, log_decay):
    core = lax.axis_index("core").astype(jnp.int32).reshape(1)
    other_core = 1 - core
    swap = [(0, 1), (1, 0)]
    tokens = (log_decay, queries, keys, values, grad_out)
    for_other = device_states(other_core, *tokens)
    from_other = lax.ppermute(for_other, "core", swap)
    own = device_states(core, *tokens)
    payload = combine(core, own, from_other)
    received = lax.all_to_all(payload.reshape(64 * 72, 128), CHIPS, 0, 0, tiled=True)
    prefixes = scan_chips(received.reshape(64, 72, 128))
    back = lax.all_to_all(prefixes.reshape(64 * 64, 128), CHIPS, 0, 0, tiled=True)
    keep, send = middle(core, back.reshape(64, 64, 128), own, from_other)
    arrived = lax.ppermute(send, "core", swap)
    started = gradients(core, *tokens, keep)
    return tuple(gradients(other_core, *tokens, arrived, started))


def solution(mesh):
    torus = Mesh(mesh.devices.reshape(4, 4, 4, 2), ALL)
    rows = P(ALL, None)
    return jax.shard_map(
        body,
        mesh=torus,
        in_specs=(rows, rows, rows, rows, P(None, ALL)),
        out_specs=(rows, rows, rows),
        check_vma=False,
    )
```

time: 246 us -> 120 us (0.49)
  waiting for transfers between devices: 96.4 us -> 0.01 us
  blocking collectives: 27.9 us -> 78 us
  Pallas kernels: 0 us -> 34.2 us
  other arithmetic: 31.9 us -> 0 us
  local copies, waits for them, and re-layouts: 31.4 us -> 2.66 us
  starting transfers between devices: 28.1 us -> 3.95 us
  matrix products: 15.4 us -> 0 us
  between operations: 14.1 us -> 0.66 us
    all_to_all x0 -> x2, blocking collectives: none -> 78 us  [the longest x1 43.9 us: body(): lax.all_to_all(payload.reshape(64 * 72, 128), CHIPS, 0, 0, tiled=True)]
    all_to_all x5 -> x0, waiting for transfers between devices: 69.7 us -> none  [the longest x1 22.1 us: body(): lax.all_to_all(running[None], 'mem', split_axis=2, concat_axis=0, tiled=T...]
    pallas_call x0 -> x7, Pallas kernels: none -> 34.2 us  [the longest x2 11.4 us: gradients(): pl.pallas_call(grads_kernel, out_shape=[shape] * 3, grid_spec=pltpu.Prefe...]
    all_to_all x5 -> x0, starting transfers between devices: 28 us -> none  [the longest x1 7.01 us: body(): lax.all_to_all(second_stack, 'mem', split_axis=0, concat_axis=2, tiled=True)]
    all_gather x4 -> x0, blocking collectives: 27.9 us -> none  [entering(): pieces = jax.tree.map(lambda part: lax.all_gather(part, axis), total)]
    all_gather x4 -> x0, waiting for transfers between devices: 26.7 us -> none  [entering(): pieces = jax.tree.map(lambda part: lax.all_gather(part, axis), total)]
    unnamed x15 -> x0, other arithmetic: 18.8 us -> none
    dot_general x9 -> x0, matrix products: 15.4 us -> none  [the longest x1 3.18 us: body(): jnp.einsum('bhts,bthe->bshe', weight_value, grad_blocks, preferred_elemen...]
  transfers between devices with their start and end apart: 9 -> 2, of which waited for: 6 -> 0; matrix products, arithmetic and copies ran while one was open for 24% -> 0% of each run, Pallas kernels for 0% -> 9%
where the time goes in v1:
time: 120 us; the launch traced here: 119 us
  blocking collectives  78 us (65%)
  Pallas kernels  34.2 us (29%)
  starting transfers between devices  3.95 us (3%)
  local copies, waits for them, and re-layouts  2.66 us (2%)
    all_to_all x1, blocking collectives, body(): lax.all_to_all(payload.reshape(64 * 72, 128), CHIPS, 0, 0, tiled=True)  43.9 us
    all_to_all x1, blocking collectives, body(): lax.all_to_all(prefixes.reshape(64 * 64, 128), CHIPS, 0, 0, tiled=True)  34.1 us
    pallas_call x2, Pallas kernels, gradients(): pl.pallas_call(grads_kernel, out_shape=[shape] * 3, grid_spec=pltpu.Prefe...  11.4 us
    pallas_call x2, Pallas kernels, device_states(): pl.pallas_call(states_kernel, out_shape=jax.ShapeDtypeStruct((GROUP, STAT...  9.87 us
    pallas_call x1, Pallas kernels, middle(): pl.pallas_call(middle_kernel, out_shape=[jax.ShapeDtypeStruct((GROUP, 2 *...  5.26 us
    pallas_call x1, Pallas kernels, combine(): pl.pallas_call(combine_kernel, out_shape=jax.ShapeDtypeStruct((64, 72, 12...  4.33 us
    pallas_call x1, Pallas kernels, scan_chips(): pl.pallas_call(scan_kernel, out_shape=jax.ShapeDtypeStruct((64, 64, 128),...  3.32 us
    unnamed x4, local copies, waits for them, and re-layouts  2.66 us
  transfers between devices with their start and end apart: 2, of which 0 were waited for; matrix products, arithmetic and copies ran while one was open for 0% of the time, Pallas kernels for 9%

profile of v1, /device:TPU:1, one launch (start us, length us, event | category | flops | bytes accessed | tf_op | source)
XLA Modules:
  0.0 119.5 jit_solution(5117683121935330651)
XLA Ops:
  0.6 5.0 %device_states.3 = f32[4,520,256]{2,1,0:T(8,128)} custom-call(s32[1]{0:T(128)S(6)} %sub.3.grp_ref, f32[8,256]{1,0:T(8,128)} %log_ref.7, bf16[256,2048]{1,0:T(8,128)(2,1)} %q_ref.7, bf16[256,2048]{1,0:T(8,128)(2,1)} %k_ref.7, bf16[256,2048]{1,0:T(8,128)(2,1)} %v_ref.7, bf16[256,2048]{1,0:T(8,128)(2,1)} %g_ref.7), custom_call_target="tpu_custom_call" | custom-call | tf_op jit(solution)/shard_map/device_states/pallas_call | solution.py:72
  5.6 1.4 %collective-permute-start = (f32[4,520,256]{2,1,0:T(8,128)}, f32[4,520,256]{2,1,0:T(8,128)S(1)}, u32[]{:S(2)}, u32[]{:S(2)}) collective-permute-start(f32[4,520,256]{2,1,0:T(8,128)} %device_states.3), channel_id=1, source_target_pairs={{0,1},{1,0},{2,3},{3,2},{4,5},{5,4},{6,7},{7,6},{8,9},{9,8},{10,11... | collective-permute-start | bytes 6389768 | tf_op jit(solution)/shard_map/ppermute | solution.py:242
  7.0 4.9 %device_states.2.own_ref = f32[4,520,256]{2,1,0:T(8,128)} custom-call(s32[1]{0:T(128)} %bitcast.grp_ref.core_ref, f32[8,256]{1,0:T(8,128)} %log_ref.7, bf16[256,2048]{1,0:T(8,128)(2,1)} %q_ref.7, bf16[256,2048]{1,0:T(8,128)(2,1)} %k_ref.7, bf16[256,2048]{1,0:T(8,128)(2,1)} %v_ref.7, bf16[256,2048]{1,0:T(8,128)(2,1)} %g_ref.7), custom_call_target="tpu_custom_call" | custom-call | tf_op jit(solution)/shard_map/device_states/pallas_call | solution.py:72
  11.9 0.0 collective-permute-done.other_ref
  11.9 0.0 copy-start
  11.9 1.3 %copy-done = f32[4,520,256]{2,1,0:T(8,128)} copy-done((f32[4,520,256]{2,1,0:T(8,128)}, f32[4,520,256]{2,1,0:T(8,128)S(1)}, u32[]{:S(2)}) %copy-start) | copy-done | bytes 2129944
  13.2 4.3 %combine_cores.1 = f32[64,72,128]{2,1,0:T(8,128)} custom-call(s32[1]{0:T(128)} %bitcast.grp_ref.core_ref, f32[4,520,256]{2,1,0:T(8,128)} %device_states.2.own_ref, f32[4,520,256]{2,1,0:T(8,128)} %copy-done), custom_call_target="tpu_custom_call" | custom-call | tf_op jit(solution)/shard_map/combine_cores/pallas_call | solution.py:106
  17.5 43.9 %all_to_all.12.in_ref = f32[64,72,128]{2,1,0:T(8,128)} all-to-all(f32[64,72,128]{2,1,0:T(8,128)} %combine_cores.1), channel_id=1, replica_groups=mesh['z'=4,'y'=4,'x'=4,'core'=2] {'z','y','x'}, dimensions={0} | all-to-all | bytes 4718592 | tf_op jit(solution)/shard_map/all_to_all | solution.py:245
  61.5 3.3 %scan_chips.1 = f32[64,64,128]{2,1,0:T(8,128)} custom-call(f32[64,72,128]{2,1,0:T(8,128)} %all_to_all.12.in_ref), custom_call_target="tpu_custom_call" | custom-call | tf_op jit(solution)/shard_map/scan_chips/pallas_call | solution.py:139
  64.8 34.1 %all_to_all.13.back_ref = f32[64,64,128]{2,1,0:T(8,128)} all-to-all(f32[64,64,128]{2,1,0:T(8,128)} %scan_chips.1), channel_id=1, replica_groups=mesh['z'=4,'y'=4,'x'=4,'core'=2] {'z','y','x'}, dimensions={0} | all-to-all | bytes 4194304 | tf_op jit(solution)/shard_map/all_to_all | solution.py:247
  98.9 5.3 %middle_states.1 = (f32[4,512,256]{2,1,0:T(8,128)}, f32[4,512,256]{2,1,0:T(8,128)}) custom-call(s32[1]{0:T(128)} %bitcast.grp_ref.core_ref, f32[64,64,128]{2,1,0:T(8,128)} %all_to_all.13.back_ref, f32[4,520,256]{2,1,0:T(8,128)} %device_states.2.own_ref, f32[4,520,256]{2,1,0:T(8,128)} %copy-done), custom_call_target="tpu_custom_call" | custom-call | tf_op jit(solution)/shard_map/middle_states/pallas_call | solution.py:171
  104.1 2.6 %collective-permute-start.1 = (f32[4,512,256]{2,1,0:T(8,128)}, f32[4,512,256]{2,1,0:T(8,128)S(1)}, u32[]{:S(2)}, u32[]{:S(2)}) collective-permute-start(f32[4,512,256]{2,1,0:T(8,128)} %get-tuple-element.8), channel_id=1, source_target_pairs={{0,1},{1,0},{2,3},{3,2},{4,5},{5,4},{6,7},{7,6},{8,9},{9,8},{10,11... | collective-permute-start | bytes 6291464 | tf_op jit(solution)/shard_map/ppermute | solution.py:249
  106.7 5.7 %gradients.2 = (bf16[256,2048]{1,0:T(8,128)(2,1)}, bf16[256,2048]{1,0:T(8,128)(2,1)}, bf16[256,2048]{1,0:T(8,128)(2,1)}) custom-call(s32[1]{0:T(128)} %bitcast.grp_ref.core_ref, f32[8,256]{1,0:T(8,128)} %log_ref.7, bf16[256,2048]{1,0:T(8,128)(2,1)} %q_ref.7, bf16[256,2048]{1,0:T(8,128)(2,1)} %k_ref.7, bf16[256,2048]{1,0:T(8,128)(2,1)} %v_ref.7, ...), custom_call_target="tpu_custom_call" | custom-call | tf_op jit(solution)/shard_map/gradients/pallas_call | solution.py:218
  112.4 0.0 collective-permute-done.1.st_ref
  112.4 0.0 copy-start.1
  112.4 1.3 %copy-done.1 = f32[4,512,256]{2,1,0:T(8,128)} copy-done((f32[4,512,256]{2,1,0:T(8,128)}, f32[4,512,256]{2,1,0:T(8,128)S(1)}, u32[]{:S(2)}) %copy-start.1) | copy-done | bytes 2097176
  113.8 5.7 %gradients.3 = (bf16[256,2048]{1,0:T(8,128)(2,1)}, bf16[256,2048]{1,0:T(8,128)(2,1)}, bf16[256,2048]{1,0:T(8,128)(2,1)}) custom-call(s32[1]{0:T(128)S(6)} %sub.3.grp_ref, f32[8,256]{1,0:T(8,128)} %log_ref.7, bf16[256,2048]{1,0:T(8,128)(2,1)} %q_ref.7, bf16[256,2048]{1,0:T(8,128)(2,1)} %k_ref.7, ...), custom_call_target="tpu_custom_call", output_to_operand_aliasing={{0}: (7, {}), {1}: (8, {}), {2}: (9, {})} | custom-call | tf_op jit(solution)/shard_map/gradients/pallas_call | solution.py:218
Async XLA Ops:
  5.6 6.3 %collective-permute-start = (f32[4,520,256]{2,1,0:T(8,128)}, f32[4,520,256]{2,1,0:T(8,128)S(1)}, u32[]{:S(2)}, u32[]{:S(2)}) collective-permute-start(f32[4,520,256]{2,1,0:T(8,128)} %device_states.3), channel_id=1, source_target_pairs={{0,1},{1,0},{2,3},{3,2},{4,5},{5,4},{6,7},{7,6},{8,9},{9,8},{10,11... | collective-permute-start | bytes 6389768 | tf_op jit(solution)/shard_map/ppermute | solution.py:242
  11.9 1.3 %copy-start = (f32[4,520,256]{2,1,0:T(8,128)}, f32[4,520,256]{2,1,0:T(8,128)S(1)}, u32[]{:S(2)}) copy-start(f32[4,520,256]{2,1,0:T(8,128)S(1)} %collective-permute-done.other_ref) | copy-start | bytes 6389764
  104.1 8.3 %collective-permute-start.1 = (f32[4,512,256]{2,1,0:T(8,128)}, f32[4,512,256]{2,1,0:T(8,128)S(1)}, u32[]{:S(2)}, u32[]{:S(2)}) collective-permute-start(f32[4,512,256]{2,1,0:T(8,128)} %get-tuple-element.8), channel_id=1, source_target_pairs={{0,1},{1,0},{2,3},{3,2},{4,5},{5,4},{6,7},{7,6},{8,9},{9,8},{10,11... | collective-permute-start | bytes 6291464 | tf_op jit(solution)/shard_map/ppermute | solution.py:249
  112.4 1.3 %copy-start.1 = (f32[4,512,256]{2,1,0:T(8,128)}, f32[4,512,256]{2,1,0:T(8,128)S(1)}, u32[]{:S(2)}) copy-start(f32[4,512,256]{2,1,0:T(8,128)S(1)} %collective-permute-done.1.st_ref) | copy-start | bytes 6291460

commit v2 on v1

--- a/solution.py
+++ b/solution.py
@@ -15,6 +15,7 @@
 F32 = jnp.float32
 BF16 = jnp.bfloat16
 STATE_ROWS = 2 * D + 8
+VMEM_LIMIT = 12 * 1024 * 1024
 
 
 def dot(a, b, ca, cb):
@@ -79,6 +80,7 @@
             out_specs=pl.BlockSpec((1, STATE_ROWS, D), lambda i, grp: (i, 0, 0)),
             scratch_shapes=[pltpu.VMEM((TOK, HEADS), F32)],
         ),
+        compiler_params=pltpu.CompilerParams(vmem_limit_bytes=VMEM_LIMIT),
         name="device_states",
     )(grp, log_decay, q, k, v, g)
 
@@ -112,6 +114,7 @@
             in_specs=[state, state],
             out_specs=pl.BlockSpec((16, 72, 128), lambda i, core: (i, 0, 0)),
         ),
+        compiler_params=pltpu.CompilerParams(vmem_limit_bytes=VMEM_LIMIT),
         name="combine_cores",
     )(core, own, other)
 
@@ -141,6 +144,7 @@
         out_shape=jax.ShapeDtypeStruct((64, 64, 128), F32),
         in_specs=[pl.BlockSpec(memory_space=pltpu.VMEM)],
         out_specs=pl.BlockSpec(memory_space=pltpu.VMEM),
+        compiler_params=pltpu.CompilerParams(vmem_limit_bytes=VMEM_LIMIT),
         name="scan_chips",
     )(received)
 
@@ -177,6 +181,7 @@
             in_specs=[pl.BlockSpec((16, 64, 128), lambda i, core: (i, 0, 0)), state, state],
             out_specs=[pair, pair],
         ),
+        compiler_params=pltpu.CompilerParams(vmem_limit_bytes=VMEM_LIMIT),
         name="middle_states",
     )(core, back, own, other)
 
@@ -229,6 +234,7 @@
             scratch_shapes=[pltpu.VMEM((TOK, HEADS), F32), pltpu.VMEM((HEADS, TOK), F32)],
         ),
         input_output_aliases={7 + n: n for n in range(count)},
+        compiler_params=pltpu.CompilerParams(vmem_limit_bytes=VMEM_LIMIT),
         name="gradients",
     )(grp, log_decay, q, k, v, g, states, *started)
 

time: 120 us -> 104 us (0.87)
  Pallas kernels: 34.2 us -> 14 us
  local copies, waits for them, and re-layouts: 2.66 us -> 5.61 us
  waiting for transfers between devices: 0.01 us -> 1.46 us
    pallas_call x2, Pallas kernels: 9.87 us -> 4.72 us  [device_states(): pl.pallas_call(states_kernel, out_shape=jax.ShapeDtypeStruct((GROUP, STAT...]
    pallas_call x1, Pallas kernels: 5.26 us -> 0.66 us  [middle(): pl.pallas_call(middle_kernel, out_shape=[jax.ShapeDtypeStruct((GROUP, 2 *...]
    pallas_call x1, Pallas kernels: 4.33 us -> 0.32 us  [combine(): pl.pallas_call(combine_kernel, out_shape=jax.ShapeDtypeStruct((64, 72, 12...]
    pallas_call x2, Pallas kernels: 11.4 us -> 8.1 us  [gradients(): pl.pallas_call(grads_kernel, out_shape=[shape] * 3, grid_spec=pltpu.Prefe...]
    pallas_call x1, Pallas kernels: 3.32 us -> 0.25 us  [scan_chips(): pl.pallas_call(scan_kernel, out_shape=jax.ShapeDtypeStruct((64, 64, 128),...]
    unnamed x4 -> x20, local copies, waits for them, and re-layouts: 2.66 us -> 5.61 us
    ppermute x1, waiting for transfers between devices: 0.01 us -> 1.46 us  [body(): from_other = lax.ppermute(for_other, 'core', swap)]
  transfers between devices with their start and end apart: 2 -> 2, of which waited for: 0 -> 1; matrix products, arithmetic and copies ran while one was open for 0% -> 0% of each run, Pallas kernels for 9% -> 6%
where the time goes in v2:
time: 104 us; the launch traced here: 103 us
  blocking collectives  77.6 us (75%)
  Pallas kernels  14 us (13%)
  local copies, waits for them, and re-layouts  5.61 us (5%)
  starting transfers between devices  4.05 us (4%)
  waiting for transfers between devices  1.46 us (1%)
    all_to_all x1, blocking collectives, body(): lax.all_to_all(payload.reshape(64 * 72, 128), CHIPS, 0, 0, tiled=True)  43.5 us
    all_to_all x1, blocking collectives, body(): lax.all_to_all(prefixes.reshape(64 * 64, 128), CHIPS, 0, 0, tiled=True)  34.1 us
    pallas_call x2, Pallas kernels, gradients(): pl.pallas_call(grads_kernel, out_shape=[shape] * 3, grid_spec=pltpu.Prefe...  8.1 us
    unnamed x20, local copies, waits for them, and re-layouts  5.61 us
    pallas_call x2, Pallas kernels, device_states(): pl.pallas_call(states_kernel, out_shape=jax.ShapeDtypeStruct((GROUP, STAT...  4.72 us
    ppermute x1, starting transfers between devices, body(): arrived = lax.ppermute(send, 'core', swap)  2.59 us
  transfers between devices with their start and end apart: 2, of which 1 were waited for; matrix products, arithmetic and copies ran while one was open for 0% of the time, Pallas kernels for 6%

profile of v2, /device:TPU:1, one launch (start us, length us, event | category | flops | bytes accessed | tf_op | source)
XLA Modules:
  0.0 103.4 jit_solution(15198349913677491164)
XLA Ops:
  0.6 0.0 copy-start
  0.6 1.2 %copy-done = bf16[256,2048]{1,0:T(8,128)(2,1)S(1)} copy-done((bf16[256,2048]{1,0:T(8,128)(2,1)S(1)}, bf16[256,2048]{1,0:T(8,128)(2,1)}, u32[]{:S(2)}) %copy-start) | copy-done | bytes 1048600
  1.9 0.0 copy-start.2
  1.9 1.2 %copy-done.2 = bf16[256,2048]{1,0:T(8,128)(2,1)S(1)} copy-done((bf16[256,2048]{1,0:T(8,128)(2,1)S(1)}, bf16[256,2048]{1,0:T(8,128)(2,1)}, u32[]{:S(2)}) %copy-start.2) | copy-done | bytes 1048600
  3.1 0.0 copy-start.4
  3.1 1.2 %copy-done.4 = bf16[256,2048]{1,0:T(8,128)(2,1)S(1)} copy-done((bf16[256,2048]{1,0:T(8,128)(2,1)S(1)}, bf16[256,2048]{1,0:T(8,128)(2,1)}, u32[]{:S(2)}) %copy-start.4) | copy-done | bytes 1048600
  4.3 0.0 copy-start.6
  4.3 1.2 %copy-done.6 = bf16[256,2048]{1,0:T(8,128)(2,1)S(1)} copy-done((bf16[256,2048]{1,0:T(8,128)(2,1)S(1)}, bf16[256,2048]{1,0:T(8,128)(2,1)}, u32[]{:S(2)}) %copy-start.6) | copy-done | bytes 1048600
  5.5 0.0 copy-start.8
  5.5 0.7 copy-done.8
  6.2 0.0 copy-start.1
  6.2 0.0 copy-start.9
  6.2 2.4 %device_states.3 = f32[4,520,256]{2,1,0:T(8,128)S(1)} custom-call(s32[1]{0:T(128)S(6)} %sub.3.grp_ref, f32[8,256]{1,0:T(8,128)S(1)} %copy-done.8, bf16[256,2048]{1,0:T(8,128)(2,1)S(1)} %copy-done, bf16[256,2048]{1,0:T(8,128)(2,1)S(1)} %copy-done.2, bf16[256,2048]{1,0:T(8,128)(2,1)S(1)} %copy-done.4, bf16[256,2048]{1,0:T(8,128)(2,1)S(1)} %copy-done.6), custom_call_target="tpu_custom_call" | custom-call | tf_op jit(solution)/shard_map/device_states/pallas_call | solution.py:73
  8.6 1.5 %collective-permute-start = (f32[4,520,256]{2,1,0:T(8,128)S(1)}, f32[4,520,256]{2,1,0:T(8,128)S(1)}, u32[]{:S(2)}, u32[]{:S(2)}) collective-permute-start(f32[4,520,256]{2,1,0:T(8,128)S(1)} %device_states.3), channel_id=1, source_target_pairs={{0,1},{1,0},{2,3},{3,2},{4,5},{5,4},{6,7},{7,6},{8,9},{9,8},{10,11... | collective-permute-start | bytes 6389768 | tf_op jit(solution)/shard_map/ppermute | solution.py:248
  10.1 0.0 copy-done.1
  10.1 0.0 copy-done.9
  10.1 2.4 %device_states.2.own_ref = f32[4,520,256]{2,1,0:T(8,128)S(1)} custom-call(s32[1]{0:T(128)} %bitcast.grp_ref.core_ref, f32[8,256]{1,0:T(8,128)S(1)} %copy-done.9, bf16[256,2048]{1,0:T(8,128)(2,1)S(1)} %copy-done.1, bf16[256,2048]{1,0:T(8,128)(2,1)S(1)} %copy-done.2, bf16[256,2048]{1,0:T(8,128)(2,1)S(1)} %copy-done.4, bf16[256,2048]{1,0:T(8,128)(2,1)S(1)} %copy-done.6), custom_call_target="tpu_custom_call" | custom-call | tf_op jit(solution)/shard_map/device_states/pallas_call | solution.py:73
  12.4 1.5 %collective-permute-done.other_ref = f32[4,520,256]{2,1,0:T(8,128)S(1)} collective-permute-done((f32[4,520,256]{2,1,0:T(8,128)S(1)}, f32[4,520,256]{2,1,0:T(8,128)S(1)}, u32[]{:S(2)}, u32[]{:S(2)}) %collective-permute-start) | collective-permute-done | bytes 2129952 | tf_op jit(solution)/shard_map/ppermute | solution.py:248
  13.9 0.3 combine_cores.1
  14.2 43.5 %all_to_all.12.in_ref = f32[64,72,128]{2,1,0:T(8,128)S(1)} all-to-all(f32[64,72,128]{2,1,0:T(8,128)S(1)} %combine_cores.1), channel_id=1, replica_groups=mesh['z'=4,'y'=4,'x'=4,'core'=2] {'z','y','x'}, dimensions={0} | all-to-all | bytes 4718592 | tf_op jit(solution)/shard_map/all_to_all | solution.py:251
  57.7 0.2 scan_chips.1
  58.0 34.1 %all_to_all.13.back_ref = f32[64,64,128]{2,1,0:T(8,128)S(1)} all-to-all(f32[64,64,128]{2,1,0:T(8,128)S(1)} %scan_chips.1), channel_id=1, replica_groups=mesh['z'=4,'y'=4,'x'=4,'core'=2] {'z','y','x'}, dimensions={0} | all-to-all | bytes 4194304 | tf_op jit(solution)/shard_map/all_to_all | solution.py:253
  92.1 0.0 copy-start.3
  92.1 0.0 copy-start.5
  92.1 0.7 middle_states.1
  92.7 2.6 %collective-permute-start.1 = (f32[4,512,256]{2,1,0:T(8,128)S(1)}, f32[4,512,256]{2,1,0:T(8,128)S(1)}, u32[]{:S(2)}, u32[]{:S(2)}) collective-permute-start(f32[4,512,256]{2,1,0:T(8,128)S(1)} %get-tuple-element.8), channel_id=1, source_target_pairs={{0,1},{1,0},{2,3},{3,2},{4,5},{5,4},{6,7},{7,6},{8,9},{9,8},{10,11... | collective-permute-start | bytes 6291464 | tf_op jit(solution)/shard_map/ppermute | solution.py:255
  95.3 0.0 copy-done.3
  95.3 0.0 copy-done.5
  95.3 0.0 copy-done.7
  95.3 4.1 %gradients.2 = (bf16[256,2048]{1,0:T(8,128)(2,1)}, bf16[256,2048]{1,0:T(8,128)(2,1)}, bf16[256,2048]{1,0:T(8,128)(2,1)}) custom-call(s32[1]{0:T(128)} %bitcast.grp_ref.core_ref, f32[8,256]{1,0:T(8,128)S(1)} %copy-done.9, bf16[256,2048]{1,0:T(8,128)(2,1)S(1)} %copy-done.1, bf16[256,2048]{1,0:T(8,128)(2,1)S(1)} %copy-done.3, bf16[256,2048]{1,0:T(8,128)(2,1)S(1)} %copy-done.5, ...), custom_call_target="tpu_custom_call" | custom-call | tf_op jit(solution)/shard_map/gradients/pallas_call | solution.py:223
  99.4 0.0 collective-permute-done.1.st_ref
  99.4 4.0 %gradients.3 = (bf16[256,2048]{1,0:T(8,128)(2,1)}, bf16[256,2048]{1,0:T(8,128)(2,1)}, bf16[256,2048]{1,0:T(8,128)(2,1)}) custom-call(s32[1]{0:T(128)S(6)} %sub.3.grp_ref, f32[8,256]{1,0:T(8,128)S(1)} %copy-done.9, bf16[256,2048]{1,0:T(8,128)(2,1)S(1)} %copy-done.1, ...), custom_call_target="tpu_custom_call", output_to_operand_aliasing={{0}: (7, {}), {1}: (8, {}), {2}: (9, {})} | custom-call | tf_op jit(solution)/shard_map/gradients/pallas_call | solution.py:223
  (1 shorter events, 0.0 us)
Async XLA Ops:
  0.6 1.2 %copy-start = (bf16[256,2048]{1,0:T(8,128)(2,1)S(1)}, bf16[256,2048]{1,0:T(8,128)(2,1)}, u32[]{:S(2)}) copy-start(bf16[256,2048]{1,0:T(8,128)(2,1)} %q_ref.7) | copy-start | bytes 3145732
  1.9 1.2 %copy-start.2 = (bf16[256,2048]{1,0:T(8,128)(2,1)S(1)}, bf16[256,2048]{1,0:T(8,128)(2,1)}, u32[]{:S(2)}) copy-start(bf16[256,2048]{1,0:T(8,128)(2,1)} %k_ref.7) | copy-start | bytes 3145732
  3.1 1.2 %copy-start.4 = (bf16[256,2048]{1,0:T(8,128)(2,1)S(1)}, bf16[256,2048]{1,0:T(8,128)(2,1)}, u32[]{:S(2)}) copy-start(bf16[256,2048]{1,0:T(8,128)(2,1)} %v_ref.7) | copy-start | bytes 3145732
  4.3 1.2 %copy-start.6 = (bf16[256,2048]{1,0:T(8,128)(2,1)S(1)}, bf16[256,2048]{1,0:T(8,128)(2,1)}, u32[]{:S(2)}) copy-start(bf16[256,2048]{1,0:T(8,128)(2,1)} %g_ref.7) | copy-start | bytes 3145732
  5.5 0.7 copy-start.8
  6.2 3.8 %copy-start.1 = (bf16[256,2048]{1,0:T(8,128)(2,1)S(1)}, bf16[256,2048]{1,0:T(8,128)(2,1)}, u32[]{:S(2)}) copy-start(bf16[256,2048]{1,0:T(8,128)(2,1)} %q_ref.7) | copy-start | bytes 3145732
  6.2 3.8 %copy-start.9 = (f32[8,256]{1,0:T(8,128)S(1)}, f32[8,256]{1,0:T(8,128)}, u32[]{:S(2)}) copy-start(f32[8,256]{1,0:T(8,128)} %log_ref.7) | copy-start | bytes 24580
  8.6 5.3 %collective-permute-start = (f32[4,520,256]{2,1,0:T(8,128)S(1)}, f32[4,520,256]{2,1,0:T(8,128)S(1)}, u32[]{:S(2)}, u32[]{:S(2)}) collective-permute-start(f32[4,520,256]{2,1,0:T(8,128)S(1)} %device_states.3), channel_id=1, source_target_pairs={{0,1},{1,0},{2,3},{3,2},{4,5},{5,4},{6,7},{7,6},{8,9},{9,8},{10,11... | collective-permute-start | bytes 6389768 | tf_op jit(solution)/shard_map/ppermute | solution.py:248
  92.1 3.3 %copy-start.3 = (bf16[256,2048]{1,0:T(8,128)(2,1)S(1)}, bf16[256,2048]{1,0:T(8,128)(2,1)}, u32[]{:S(2)}) copy-start(bf16[256,2048]{1,0:T(8,128)(2,1)} %k_ref.7) | copy-start | bytes 3145732
  92.1 3.3 %copy-start.5 = (bf16[256,2048]{1,0:T(8,128)(2,1)S(1)}, bf16[256,2048]{1,0:T(8,128)(2,1)}, u32[]{:S(2)}) copy-start(bf16[256,2048]{1,0:T(8,128)(2,1)} %v_ref.7) | copy-start | bytes 3145732
  92.1 3.3 %copy-start.7 = (bf16[256,2048]{1,0:T(8,128)(2,1)S(1)}, bf16[256,2048]{1,0:T(8,128)(2,1)}, u32[]{:S(2)}) copy-start(bf16[256,2048]{1,0:T(8,128)(2,1)} %g_ref.7) | copy-start | bytes 3145732
  92.7 6.7 %collective-permute-start.1 = (f32[4,512,256]{2,1,0:T(8,128)S(1)}, f32[4,512,256]{2,1,0:T(8,128)S(1)}, u32[]{:S(2)}, u32[]{:S(2)}) collective-permute-start(f32[4,512,256]{2,1,0:T(8,128)S(1)} %get-tuple-element.8), channel_id=1, source_target_pairs={{0,1},{1,0},{2,3},{3,2},{4,5},{5,4},{6,7},{7,6},{8,9},{9,8},{10,11... | collective-permute-start | bytes 6291464 | tf_op jit(solution)/shard_map/ppermute | solution.py:255
